TPU v7x, 32 devices: a whole 2x2x4 slice. The times are simulated.
32 devices in a mesh: groups: 2 (over x), attn: 4 (over y, core), expert: 4 (over z).
Axes of the slice: x: 2, y: 2, z: 4, core: 2. Of those that a mesh axis runs over, the one named last changes fastest.
Arguments:
- tokens: bfloat16 [1024, 4096], P(('groups', 'attn'), 'expert'), parts along dimension 0, may hold values from -6 to 6
- expert_ids: int32 [1024, 8], P(('groups', 'attn')), parts along dimension 0, may hold values from 0 to 15, all different within a row; in each aligned block of 128 rows (0 to 127, 128 to 255, ...) at most 128 rows name the same one
- gate_weight: bfloat16 [1024, 8], P(('groups', 'attn')), parts along dimension 0, may hold values from 0.049804688 to 0.29882812
- w_gate: bfloat16 [16, 4096, 768], P('attn', 'expert'), may hold values from -0.09375 to 0.09375
- w_up: bfloat16 [16, 4096, 768], P('attn', 'expert'), may hold values from -0.09375 to 0.09375
- w_down: bfloat16 [16, 768, 4096], P('attn', None, 'expert'), may hold values from -0.21875 to 0.21875
- query: bfloat16 [64, 64, 128], P(('groups', 'attn', 'expert')), parts along dimension 0, may hold values from -100 to 100
- cache_k: bfloat16 [64, 768, 4, 128], P(('groups', 'attn', 'expert')), parts along dimension 0, may hold values from -6 to 6
- cache_v: bfloat16 [64, 768, 4, 128], P(('groups', 'attn', 'expert')), parts along dimension 0, may hold values from -6 to 6
- lengths: int32 [64], P(('groups', 'attn', 'expert')), parts along dimension 0, may hold values from 2 to 768, as said below
Outputs:
- moe_out: bfloat16 [1024, 4096], P(('groups', 'attn'), 'expert'), parts along dimension 0
- attn_out: bfloat16 [64, 8192], P(('groups', 'attn', 'expert')), parts along dimension 0
There are 2 independent parts, one for each index of `groups`. A program takes and returns all parts, laid end to end along the dimension named above; an argument that names none is the same for every part. Nothing has to cross between parts.
Inputs may be any that keep to these rules, and one draw needn't show every extreme that they name: `expert_ids`: each row names 8 different experts. In the rows of one index of attn (aligned blocks of 128 rows) no expert is named by more than 128 rows, and in some block some expert by exactly 128. `lengths`: some sequence has all 768 positions live.
All inputs are finite; a program needn't handle non-finite values.
Results may differ from a plain program's by a relative error of at most 0.025.
Values may be sent and summed in bfloat16 or wider, within the bound.
A program may use at most 64 MiB of HBM per device.

v0:
```python
import functools

import jax
import jax.numpy as jnp
from jax import lax
from jax.experimental import pallas as pl
from jax.experimental.pallas import tpu as pltpu
from jax.sharding import PartitionSpec as P

F32 = jnp.float32
BF16 = jnp.bfloat16


def remote(src, dst, send_sem, recv_sem, axis, peer):
    return pltpu.make_async_remote_copy(
        src_ref=src,
        dst_ref=dst,
        send_sem=send_sem,
        recv_sem=recv_sem,
        device_id={axis: peer},
        device_id_type=pl.DeviceIdType.MESH,
    )


def attend(length_ref, query_ref, ck_ref, cv_ref, att_ref, kv_count):
    seqs, heads, size = query_ref.shape
    span = ck_ref.shape[1]
    column = lax.broadcasted_iota(jnp.int32, (heads, span), 1)
    row = lax.broadcasted_iota(jnp.int32, (heads, span), 0)
    own = lax.rem(column, kv_count) == row // (heads // kv_count)
    for s in range(seqs):
        scores = lax.dot_general(
            query_ref[s], ck_ref[s], (((1,), (1,)), ((), ())),
            preferred_element_type=F32,
        ) * size ** (-0.5)
        live = own & (column < length_ref[s] * kv_count)
        masked = jnp.where(live, scores, -jnp.inf)
        peak = jnp.max(masked, axis=1, keepdims=True)
        weighted = jnp.exp(masked - peak)
        prob = (weighted / jnp.sum(weighted, axis=1, keepdims=True)).astype(BF16)
        att_ref[s] = jnp.dot(prob, cv_ref[s], preferred_element_type=F32).astype(BF16)


def moe_kernel(
    n_attn,
    n_exp,
    experts,
    kv_count,
    tok_ref,
    meta_ref,
    wg_hbm,
    wu_hbm,
    wd_hbm,
    length_ref,
    query_ref,
    ck_hbm,
    cv_hbm,
    out_ref,
    att_ref,
    wg,
    wu,
    wd,
    ck,
    cv,
    tok_all,
    meta_all,
    pos_col,
    pos_row,
    part,
    pair_in,
    part_in,
    hid,
    acc,
    ret,
    ret_in,
    w_sem,
    c_sem,
    tok_s,
    tok_r,
    meta_s,
    meta_r,
    pair_s,
    pair_r,
    part_s,
    part_r,
    hid_s,
    hid_r,
    back_s,
    back_r,
    ret_s,
    ret_r,
):
    me = lax.axis_index("attn")
    mine = lax.axis_index("expert")
    local = wg.shape[0]
    rows = tok_ref.shape[0]
    feat = tok_ref.shape[1]
    width = meta_ref.shape[1]
    ffn = wg.shape[2]
    pairs, half, slots = part.shape[1:4]
    side = lax.rem(mine, pairs)
    place_in_half = mine // pairs
    capacity = n_exp * slots
    all_rows = n_attn * rows

    def weight_copy(i, j):
        src, dst = ((wg_hbm, wg), (wu_hbm, wu), (wd_hbm, wd))[i]
        return pltpu.make_async_copy(src.at[j], dst.at[j], w_sem.at[i, j])

    for j in range(local):
        weight_copy(0, j).start()
        weight_copy(1, j).start()
    for j in range(local):
        weight_copy(2, j).start()

    ck_copy = pltpu.make_async_copy(ck_hbm, ck, c_sem.at[0])
    cv_copy = pltpu.make_async_copy(cv_hbm, cv, c_sem.at[1])
    ck_copy.start()
    cv_copy.start()

    barrier = pltpu.get_barrier_semaphore()
    for d in range(1, n_attn):
        pl.semaphore_signal(
            barrier, inc=1, device_id={"attn": lax.rem(me + d, n_attn)},
            device_id_type=pl.DeviceIdType.MESH,
        )
    for d in range(1, n_exp):
        pl.semaphore_signal(
            barrier, inc=1, device_id={"expert": lax.rem(mine + d, n_exp)},
            device_id_type=pl.DeviceIdType.MESH,
        )
    pl.semaphore_wait(barrier, n_attn + n_exp - 2)

    def meta_copy(d, slot):
        return remote(meta_ref, meta_all.at[slot], meta_s.at[d - 1], meta_r.at[d - 1],
                      "attn", lax.rem(me + d, n_attn))

    def tok_copy(d, slot):
        return remote(tok_ref, tok_all.at[slot], tok_s.at[d - 1], tok_r.at[d - 1],
                      "attn", lax.rem(me + d, n_attn))

    for d in range(1, n_attn):
        meta_copy(d, me).start()
    for d in range(1, n_attn):
        tok_copy(d, me).start()
    tok_all[me] = tok_ref[...]
    meta_all[me] = meta_ref[...]
    for d in range(1, n_attn):
        meta_copy(d, lax.rem(me + n_attn - d, n_attn)).wait_recv()

    below = (
        lax.broadcasted_iota(jnp.int32, (rows, rows), 0)
        > lax.broadcasted_iota(jnp.int32, (rows, rows), 1)
    ).astype(F32).astype(BF16)
    offset = jnp.zeros((1, width), F32)
    for b in range(n_attn):
        block = meta_all[b]
        place = jnp.dot(below, block, preferred_element_type=F32) + offset
        wide = block.astype(F32)
        offset = offset + jnp.sum(wide, axis=0, keepdims=True)
        place = jnp.where(wide > 0.5, place, -1.0)
        pos_col[b] = place
        pos_row[:, b * rows:(b + 1) * rows] = place.T

    for d in range(1, n_attn):
        tok_copy(d, lax.rem(me + n_attn - d, n_attn)).wait_recv()

    def pair_copy(j):
        return remote(part.at[j, 1 - side], pair_in.at[j], pair_s.at[j], pair_r.at[j],
                      "expert", mine + 1 - 2 * side)

    def part_copy(j, d):
        other = lax.rem(place_in_half + d, half)
        return remote(part.at[j, side, other], part_in.at[j, d - 1], part_s.at[j, d - 1],
                      part_r.at[j, d - 1], "expert", other * pairs + side)

    def hid_copy(j, d, slot):
        other = lax.rem(place_in_half + d, half)
        return remote(hid.at[j, side, place_in_half], hid.at[j, side, slot],
                      hid_s.at[j, d - 1], hid_r.at[j, d - 1], "expert",
                      other * pairs + side)

    def hid_arrive(j):
        for d in range(1, half):
            hid_copy(j, d, lax.rem(place_in_half + half - d, half)).wait_recv()

    def back_copy(j, which):
        return remote(hid.at[j, side], hid.at[j, which], back_s.at[j], back_r.at[j],
                      "expert", mine + 1 - 2 * side)

    def first(j):
        place = pos_row[pl.ds(me * local + j, 1), :].astype(jnp.int32)
        chosen = lax.broadcasted_iota(jnp.int32, (capacity, all_rows), 0) == place
        packed = jnp.dot(
            chosen.astype(F32).astype(BF16),
            tok_all[...].reshape(all_rows, feat),
            preferred_element_type=F32,
        ).astype(BF16)
        weight_copy(0, j).wait()
        weight_copy(1, j).wait()
        gate = jnp.dot(packed, wg[j], preferred_element_type=F32).astype(BF16)
        part[j, :, :, :, :ffn] = gate.reshape(pairs, half, slots, ffn)
        up = jnp.dot(packed, wu[j], preferred_element_type=F32).astype(BF16)
        part[j, :, :, :, ffn:] = up.reshape(pairs, half, slots, ffn)
        if pairs > 1:
            pair_copy(j).start()

    def reduce_pair(j):
        if pairs > 1:
            pair_copy(j).wait_recv()
            part[j, side] = (part[j, side].astype(F32) + pair_in[j].astype(F32)).astype(BF16)
        for d in range(1, half):
            part_copy(j, d).start()

    def second(j):
        for d in range(1, half):
            part_copy(j, d).wait_recv()
        both = part[j, side, place_in_half].astype(F32)
        for d in range(1, half):
            both = both + part_in[j, d - 1].astype(F32)
        gate = both[:, :ffn]
        hid[j, side, place_in_half] = (
            gate / (1.0 + jnp.exp(-gate)) * both[:, ffn:]
        ).astype(BF16)
        for d in range(1, half):
            hid_copy(j, d, place_in_half).start()

    def pass_on(j):
        hid_arrive(j)
        if pairs > 1:
            back_copy(j, side).start()

    acc[...] = jnp.zeros_like(acc)

    def third(j):
        if pairs > 1:
            back_copy(j, 1 - side).wait_recv()
        weight_copy(2, j).wait()
        result = jnp.dot(
            hid[j].reshape(capacity, ffn), wd[j], preferred_element_type=F32
        ).astype(BF16)
        column = me * local + j
        lanes = lax.broadcasted_iota(jnp.int32, (rows, width), 1)
        slot_ids = lax.broadcasted_iota(jnp.int32, (rows, capacity), 1)

        def combine(b, inner):
            place = jnp.sum(
                jnp.where(lanes == column, pos_col[b], 0.0), axis=1, keepdims=True
            ).astype(jnp.int32)
            factor = jnp.sum(
                jnp.where(lanes == column + experts, meta_all[b].astype(F32), 0.0),
                axis=1, keepdims=True,
            )
            spread = jnp.where(slot_ids == place, factor, 0.0).astype(BF16)
            acc[b] = acc[b] + jnp.dot(spread, result, preferred_element_type=F32)
            return inner

        for b in range(n_attn):
            combine(b, 0)

    def step(s, carry):
        for lag, stage in enumerate((first, reduce_pair, second, pass_on, third)):
            if lag == 2:
                @pl.when(s == 1)
                def _():
                    attend(length_ref, query_ref, ck, cv, att_ref, kv_count)

            @pl.when((s >= lag) & (s < local + lag))
            def _():
                stage(s - lag)
        return carry

    ck_copy.wait()
    cv_copy.wait()
    lax.fori_loop(0, local + 4, step, 0)

    ret[...] = acc[...].astype(BF16)

    def ret_copy(d):
        peer = lax.rem(me + d, n_attn)
        return remote(ret.at[peer], ret_in.at[d - 1], ret_s.at[d - 1], ret_r.at[d - 1],
                      "attn", peer)

    for d in range(1, n_attn):
        ret_copy(d).start()
    total = acc[me]
    for d in range(1, n_attn):
        ret_copy(d).wait_recv()
        total = total + ret_in[d - 1].astype(F32)
    out_ref[...] = total.astype(BF16)

    for d in range(1, n_attn):
        meta_copy(d, me).wait_send()
        tok_copy(d, me).wait_send()
        ret_copy(d).wait_send()

    def drain(j, carry):
        if pairs > 1:
            pair_copy(j).wait_send()
            back_copy(j, side).wait_send()
        for d in range(1, half):
            part_copy(j, d).wait_send()
            hid_copy(j, d, place_in_half).wait_send()
        return carry

    lax.fori_loop(0, local, drain, 0)


def routed(tokens, expert_ids, gate_weight, w_gate, w_up, w_down, query, cache_k, cache_v, lengths, n_attn, n_exp):
    rows, feat = tokens.shape
    local, _, ffn = w_gate.shape
    feat_out = w_down.shape[2]
    experts = local * n_attn
    capacity = rows * expert_ids.shape[1] // local
    slots = capacity // n_exp
    pairs = 2 if n_exp > 2 and n_exp % 2 == 0 else 1
    half = n_exp // pairs
    width = -(-2 * experts // 128) * 128
    wanted = jnp.arange(width, dtype=jnp.int32)[None, None, :]
    ids = expert_ids[:, :, None]
    gates = gate_weight.astype(F32)[:, :, None]
    meta = jnp.sum(
        jnp.where(ids == wanted, 1.0, jnp.where(ids + experts == wanted, gates, 0.0)),
        axis=1,
    ).astype(BF16)
    seqs, heads, size = query.shape
    context, kv_count = cache_k.shape[1:3]
    flat = (seqs, context * kv_count, size)
    dma = pltpu.SemaphoreType.DMA
    vmem = pltpu.VMEM
    return pl.pallas_call(
        functools.partial(moe_kernel, n_attn, n_exp, experts, kv_count),
        out_shape=(
            jax.ShapeDtypeStruct((rows, feat_out), BF16),
            jax.ShapeDtypeStruct(query.shape, BF16),
        ),
        in_specs=[pl.BlockSpec(memory_space=pltpu.VMEM)] * 2
        + [pl.BlockSpec(memory_space=pl.ANY)] * 3
        + [pl.BlockSpec(memory_space=pltpu.SMEM)]
        + [pl.BlockSpec(memory_space=pltpu.VMEM)]
        + [pl.BlockSpec(memory_space=pl.ANY)] * 2,
        out_specs=[pl.BlockSpec(memory_space=pltpu.VMEM)] * 2,
        scratch_shapes=[
            vmem(w_gate.shape, BF16),
            vmem(w_up.shape, BF16),
            vmem(w_down.shape, BF16),
            vmem(flat, BF16),
            vmem(flat, BF16),
            vmem((n_attn, rows, feat), BF16),
            vmem((n_attn, rows, width), BF16),
            vmem((n_attn, rows, width), F32),
            vmem((width, n_attn * rows), F32),
            vmem((local, pairs, half, slots, 2 * ffn), BF16),
            vmem((local, half, slots, 2 * ffn), BF16),
            vmem((local, half - 1, slots, 2 * ffn), BF16),
            vmem((local, pairs, half, slots, ffn), BF16),
            vmem((n_attn, rows, feat_out), F32),
            vmem((n_attn, rows, feat_out), BF16),
            vmem((n_attn - 1, rows, feat_out), BF16),
            dma((3, local)),
            dma((2,)),
            dma((n_attn - 1,)),
            dma((n_attn - 1,)),
            dma((n_attn - 1,)),
            dma((n_attn - 1,)),
            dma((local,)),
            dma((local,)),
            dma((local, half - 1)),
            dma((local, half - 1)),
            dma((local, half - 1)),
            dma((local, half - 1)),
            dma((local,)),
            dma((local,)),
            dma((n_attn - 1,)),
            dma((n_attn - 1,)),
        ],
        compiler_params=pltpu.CompilerParams(
            collective_id=0, has_side_effects=True, vmem_limit_bytes=52 * 1024 * 1024
        ),
    )(
        tokens, meta, w_gate, w_up, w_down, lengths, query,
        cache_k.reshape(flat), cache_v.reshape(flat),
    )


def body(tokens, expert_ids, gate_weight, w_gate, w_up, w_down, query, cache_k, cache_v, lengths):
    n_attn = lax.axis_size("attn")
    n_exp = lax.axis_size("expert")
    moe_out, attended = routed(
        tokens, expert_ids, gate_weight, w_gate, w_up, w_down,
        query, cache_k, cache_v, lengths, n_attn, n_exp,
    )
    attn_out = attended.reshape(query.shape[0], -1)
    return (moe_out, attn_out)


def solution(mesh):
    return jax.shard_map(
        body,
        mesh=mesh,
        in_specs=(
            P(("groups", "attn"), "expert"),
            P(("groups", "attn"), None),
            P(("groups", "attn"), None),
            P("attn", "expert", None),
            P("attn", "expert", None),
            P("attn", None, "expert"),
            P(("groups", "attn", "expert"), None, None),
            P(("groups", "attn", "expert"), None, None, None),
            P(("groups", "attn", "expert"), None, None, None),
            P(("groups", "attn", "expert")),
        ),
        out_specs=(P(("groups", "attn"), "expert"), P(("groups", "attn", "expert"), None)),
        check_vma=False,
    )
```

profile of v0, /device:TPU:1, one launch (start us, length us, event | category | flops | bytes accessed | tf_op | source)
XLA Modules:
  0.0 113.2 jit_solution(14589166979852905383)
XLA Ops:
  0.6 0.7 broadcast_add_fusion
  1.3 0.1 copy.16
  1.4 0.8 copy.17
  2.2 0.8 copy.15
  3.0 0.8 select_reduce_fusion.meta_ref
  3.8 0.0 copy-start
  3.8 0.9 copy-done
  4.7 0.0 copy-start.1
  4.7 0.8 copy-done.1
  5.5 0.0 copy-start.2
  5.5 0.7 copy-done.2
  6.1 105.7 %shard_map.113 = (bf16[128,1024]{1,0:T(8,128)(2,1)S(1)}, bf16[2,64,128]{2,1,0:T(8,128)(2,1)S(1)}) custom-call(bf16[128,1024]{1,0:T(8,128)(2,1)S(1)} %copy-done, bf16[128,128]{1,0:T(8,128)(2,1)S(1)} %select_reduce_fusion.meta_ref, bf16[4,1024,768]{2,1,0:T(8,128)(2,1)} %wg_hbm.1, bf16[4,1024,768]{2,1,0:T(8,128)(2,1)} %wu_hbm.1, bf16[4,768,1024]{2,1,0:T(8,128)(2,1)} %wd_hbm.1, ...), custom_call_target="tpu_custom_call" | custom-call | tf_op jit(solution)/shard_map/pallas_call | solution.py:331
  111.8 0.6 copy.20
  112.5 0.7 copy.22
Async XLA Ops:
  3.8 1.0 copy-start
  4.7 0.8 copy-start.1
  5.5 0.7 copy-start.2
where the time goes:
time: 114 us; the launch traced here: 113 us
  Pallas kernels  106 us (93%)
  local copies, waits for them, and re-layouts  5.38 us (5%)
  other arithmetic  1.45 us (1%)
    pallas_call x1, Pallas kernels, routed(): pl.pallas_call(functools.partial(moe_kernel, n_attn, n_exp, experts, kv_c...  106 us
    unnamed x9, local copies, waits for them, and re-layouts  4.5 us

commit v1 on v0

v1 whole, which is shorter than its diff:
```python
import functools

import jax
import jax.numpy as jnp
from jax import lax
from jax.experimental import pallas as pl
from jax.experimental.pallas import tpu as pltpu
from jax.sharding import PartitionSpec as P

F32 = jnp.float32
BF16 = jnp.bfloat16
I32 = jnp.int32

TOKEN_CUTS = 4
CHUNK_ROWS = 16
LAG = 3
RETURN_CUTS = 4


def remote(src, dst, send_sem, recv_sem, axis, peer):
    return pltpu.make_async_remote_copy(
        src_ref=src,
        dst_ref=dst,
        send_sem=send_sem,
        recv_sem=recv_sem,
        device_id={axis: peer},
        device_id_type=pl.DeviceIdType.MESH,
    )


def attend(s, length, query_ref, ck_ref, cv_ref, att_ref, kv_count):
    _, heads, size = query_ref.shape
    span = ck_ref.shape[1]
    column = lax.broadcasted_iota(I32, (heads, span), 1)
    row = lax.broadcasted_iota(I32, (heads, span), 0)
    own = lax.rem(column, kv_count) == row // (heads // kv_count)
    scores = lax.dot_general(
        query_ref[s], ck_ref[s], (((1,), (1,)), ((), ())),
        preferred_element_type=F32,
    ) * size ** (-0.5)
    live = own & (column < length * kv_count)
    masked = jnp.where(live, scores, -jnp.inf)
    peak = jnp.max(masked, axis=1, keepdims=True)
    weighted = jnp.exp(masked - peak)
    prob = (weighted / jnp.sum(weighted, axis=1, keepdims=True)).astype(BF16)
    att_ref[s] = jnp.dot(prob, cv_ref[s], preferred_element_type=F32).astype(BF16)


def moe_kernel(
    n_attn,
    n_exp,
    experts,
    kv_count,
    tok_hbm,
    ids_hbm,
    gw_hbm,
    wg_hbm,
    wu_hbm,
    wd_hbm,
    length_hbm,
    query_hbm,
    ck_hbm,
    cv_hbm,
    out_ref,
    att_ref,
    wg,
    wu,
    wd,
    ck,
    cv,
    query,
    length,
    tok_all,
    ids_all,
    gw_all,
    pos,
    gate_of,
    part,
    part_in,
    hid,
    acc,
    ret1,
    ret1_in,
    ret2,
    ret2_in,
    w_sem,
    c_sem,
    ids_s,
    ids_r,
    gw_s,
    gw_r,
    far_s,
    far_r,
    near_s,
    near_r,
    part_s,
    part_r,
    hid_s,
    hid_r,
    ret1_s,
    ret1_r,
    ret2_s,
    ret2_r,
):
    me = lax.axis_index("attn")
    mine = lax.axis_index("expert")
    lane = lax.rem(me, 2)
    line = me // 2
    lines = n_attn // 2
    partner = me + 1 - 2 * lane
    last = n_exp - 1
    local = wg.shape[0]
    rows, feat = tok_all.shape[1:]
    ffn = wg.shape[2]
    feat_out = wd.shape[2]
    topk = ids_all.shape[1]
    half = part.shape[2]
    capacity = 2 * half
    all_rows = n_attn * rows
    per = half // CHUNK_ROWS
    chunks = local * per
    cut = feat // TOKEN_CUTS
    out_cut = feat_out // RETURN_CUTS

    def at_line(other):
        return lax.rem(other + 2 * lines, lines)

    tok_copy = pltpu.make_async_copy(tok_hbm, tok_all.at[me], c_sem.at[0])
    ids_copy = pltpu.make_async_copy(ids_hbm, ids_all.at[me], c_sem.at[1])
    gw_copy = pltpu.make_async_copy(gw_hbm, gw_all.at[me], c_sem.at[2])
    len_copy = pltpu.make_async_copy(length_hbm, length, c_sem.at[3])
    query_copy = pltpu.make_async_copy(query_hbm, query, c_sem.at[4])
    ck_copy = pltpu.make_async_copy(ck_hbm, ck, c_sem.at[5])
    cv_copy = pltpu.make_async_copy(cv_hbm, cv, c_sem.at[6])
    for copy in (ids_copy, gw_copy, tok_copy, len_copy, query_copy, ck_copy, cv_copy):
        copy.start()

    def weight_copy(i, j):
        src, dst = ((wg_hbm, wg), (wu_hbm, wu), (wd_hbm, wd))[i]
        return pltpu.make_async_copy(src.at[j], dst.at[j], w_sem.at[i, j])

    for j in range(local):
        weight_copy(0, j).start()
        weight_copy(1, j).start()
    for j in range(local):
        weight_copy(2, j).start()

    barrier = pltpu.get_barrier_semaphore()
    for d in range(1, n_attn):
        pl.semaphore_signal(
            barrier, inc=1, device_id={"attn": lax.rem(me + d, n_attn)},
            device_id_type=pl.DeviceIdType.MESH,
        )

    @pl.when(mine > 0)
    def _():
        pl.semaphore_signal(
            barrier, inc=1, device_id={"expert": mine - 1},
            device_id_type=pl.DeviceIdType.MESH,
        )

    @pl.when(mine < last)
    def _():
        pl.semaphore_signal(
            barrier, inc=1, device_id={"expert": mine + 1},
            device_id_type=pl.DeviceIdType.MESH,
        )

    ends = jnp.where(mine > 0, 1, 0) + jnp.where(mine < last, 1, 0)
    ids_copy.wait()
    gw_copy.wait()
    tok_copy.wait()
    pl.semaphore_wait(barrier, n_attn - 1 + ends)

    def ids_send(d, slot):
        return remote(ids_all.at[slot], ids_all.at[slot], ids_s.at[d - 1], ids_r.at[d - 1],
                      "attn", lax.rem(me + d, n_attn))

    def gw_send(d, slot):
        return remote(gw_all.at[slot], gw_all.at[slot], gw_s.at[d - 1], gw_r.at[d - 1],
                      "attn", lax.rem(me + d, n_attn))

    def far(d, q, block):
        view = tok_all.at[block, :, pl.ds(q * cut, cut)]
        return remote(view, view, far_s.at[d - 1, q], far_r.at[d - 1, q],
                      "attn", at_line(line + d) * 2 + lane)

    def near(d, q, block):
        view = tok_all.at[block, :, pl.ds(q * cut, cut)]
        return remote(view, view, near_s.at[d, q], near_r.at[d, q], "attn", partner)

    def sender(d):
        return at_line(line - d) * 2 + lane

    for d in range(1, n_attn):
        ids_send(d, me).start()
        gw_send(d, me).start()
    for q in range(TOKEN_CUTS):
        for d in range(1, lines):
            far(d, q, me).start()
    for q in range(TOKEN_CUTS):
        near(0, q, me).start()

    acc[...] = jnp.zeros_like(acc)

    for d in range(1, n_attn):
        ids_send(d, lax.rem(me + n_attn - d, n_attn)).wait_recv()
        gw_send(d, lax.rem(me + n_attn - d, n_attn)).wait_recv()

    before = (
        lax.broadcasted_iota(I32, (rows, rows), 0)
        < lax.broadcasted_iota(I32, (rows, rows), 1)
    ).astype(F32).astype(BF16)
    names = lax.broadcasted_iota(I32, (experts, rows), 0)
    offset = jnp.zeros((experts, 1), F32)
    for b in range(n_attn):
        member = jnp.zeros((experts, rows), F32)
        factor = jnp.zeros((experts, rows), F32)
        wide = gw_all[b].astype(F32)
        for k in range(topk):
            hit = names == ids_all[b, k:k + 1, :]
            member = jnp.where(hit, 1.0, member)
            factor = jnp.where(hit, wide[k:k + 1, :], factor)
        place = jnp.dot(member.astype(BF16), before, preferred_element_type=F32) + offset
        offset = offset + jnp.sum(member, axis=1, keepdims=True)
        pos[:, b * rows:(b + 1) * rows] = jnp.where(member > 0.5, place, -1.0).astype(I32)
        gate_of[:, b * rows:(b + 1) * rows] = factor

    len_copy.wait()
    query_copy.wait()
    ck_copy.wait()
    cv_copy.wait()
    relay = [(d, q) for q in range(TOKEN_CUTS) for d in range(1, lines)]
    seqs = query.shape[0]
    done = 0
    for s in range(seqs):
        attend(s, length[s], query, ck, cv, att_ref, kv_count)
        until = len(relay) * (s + 1) // (seqs + 1)
        for d, q in relay[done:until]:
            far(d, q, sender(d)).wait_recv()
            near(d, q, sender(d)).start()
        done = until
    for d, q in relay[done:]:
        far(d, q, sender(d)).wait_recv()
        near(d, q, sender(d)).start()
    for q in range(TOKEN_CUTS):
        for d in range(lines):
            near(d, q, at_line(line - d) * 2 + 1 - lane).wait_recv()

    def steps_from(way):
        return mine if way == 0 else last - mine

    def piece(ref, way, k):
        j = k // per
        first_row = pl.multiple_of(lax.rem(k, per) * CHUNK_ROWS, CHUNK_ROWS)
        return ref.at[j, way, pl.ds(first_row, CHUNK_ROWS)]

    def part_copy(way, k):
        return remote(piece(part, way, k), piece(part_in, way, k),
                      part_s.at[way, k // per], part_r.at[way, k],
                      "expert", lax.rem(mine + 1 - 2 * way + n_exp, n_exp))

    def hid_copy(way, k):
        return remote(piece(hid, way, k), piece(hid, way, k),
                      hid_s.at[way, k // per], hid_r.at[way, k],
                      "expert", lax.rem(mine - 1 + 2 * way + n_exp, n_exp))

    def first(j, carry):
        place = pos[pl.ds(me * local + j, 1), :]
        chosen = lax.broadcasted_iota(I32, (capacity, all_rows), 0) == place
        packed = jnp.dot(
            chosen.astype(F32).astype(BF16),
            tok_all[...].reshape(all_rows, feat),
            preferred_element_type=F32,
        ).astype(BF16)
        weight_copy(0, j).wait()
        weight_copy(1, j).wait()
        gate = jnp.dot(packed, wg[j], preferred_element_type=F32).astype(BF16)
        part[j, :, :, :ffn] = gate.reshape(2, half, ffn)
        up = jnp.dot(packed, wu[j], preferred_element_type=F32).astype(BF16)
        part[j, :, :, ffn:] = up.reshape(2, half, ffn)
        for way in range(2):
            @pl.when(steps_from(way) == 0)
            def _():
                for r in range(per):
                    part_copy(way, j * per + r).start()
        return carry

    lax.fori_loop(0, local, first, 0)

    def reduce(way, k):
        part_copy(way, k).wait_recv()
        total = piece(part, way, k)[...].astype(F32) + piece(part_in, way, k)[...].astype(F32)

        @pl.when(steps_from(way) < last)
        def _():
            piece(part, way, k)[...] = total.astype(BF16)
            part_copy(way, k).start()

        @pl.when(steps_from(way) == last)
        def _():
            gate = total[:, :ffn]
            piece(hid, way, k)[...] = (
                gate / (1.0 + jnp.exp(-gate)) * total[:, ffn:]
            ).astype(BF16)
            hid_copy(way, k).start()

    def reduce_step(s, carry):
        for way in range(2):
            k = s - LAG * (steps_from(way) - 1)

            @pl.when((steps_from(way) > 0) & (k >= 0) & (k < chunks))
            def _():
                reduce(way, k)
        return carry

    lax.fori_loop(0, chunks + LAG * (last - 1), reduce_step, 0)

    def pass_on(k, carry):
        for way in range(2):
            @pl.when(steps_from(way) < last)
            def _():
                hid_copy(way, k).wait_recv()

            @pl.when((steps_from(way) < last) & (steps_from(way) > 0))
            def _():
                hid_copy(way, k).start()
        return carry

    def second(j, carry):
        lax.fori_loop(j * per, (j + 1) * per, pass_on, 0)
        weight_copy(2, j).wait()
        result = jnp.dot(
            hid[j].reshape(capacity, ffn), wd[j], preferred_element_type=F32
        ).astype(BF16)
        place = pos[pl.ds(me * local + j, 1), :]
        factor = gate_of[pl.ds(me * local + j, 1), :]
        slots = lax.broadcasted_iota(I32, (capacity, all_rows), 0)
        spread = jnp.where(slots == place, factor, 0.0).astype(BF16)
        acc[...] += lax.dot_general(
            spread, result, (((0,), (0,)), ((), ())), preferred_element_type=F32
        )
        return carry

    lax.fori_loop(0, local, second, 0)

    def block(index, q):
        return acc[pl.ds(pl.multiple_of(index * rows, rows), rows), q * out_cut:(q + 1) * out_cut]

    def ret1_copy(q):
        columns = pl.ds(q * out_cut, out_cut)
        return remote(ret1.at[:, :, columns], ret1_in.at[:, :, columns],
                      ret1_s.at[q], ret1_r.at[q], "attn", partner)

    def ret2_copy(d, q):
        columns = pl.ds(q * out_cut, out_cut)
        return remote(ret2.at[d - 1, :, columns], ret2_in.at[d - 1, :, columns],
                      ret2_s.at[d - 1, q], ret2_r.at[d - 1, q],
                      "attn", at_line(line + d) * 2 + lane)

    for q in range(RETURN_CUTS):
        columns = slice(q * out_cut, (q + 1) * out_cut)
        for y in range(lines):
            ret1[y, :, columns] = block(2 * y + 1 - lane, q).astype(BF16)
        ret1_copy(q).start()
    for q in range(RETURN_CUTS):
        columns = slice(q * out_cut, (q + 1) * out_cut)
        ret1_copy(q).wait_recv()
        for d in range(1, lines):
            to = at_line(line + d)
            ret2[d - 1, :, columns] = (
                block(2 * to + lane, q) + ret1_in[to, :, columns].astype(F32)
            ).astype(BF16)
            ret2_copy(d, q).start()
    for q in range(RETURN_CUTS):
        columns = slice(q * out_cut, (q + 1) * out_cut)
        total = block(me, q) + ret1_in[line, :, columns].astype(F32)
        for d in range(1, lines):
            ret2_copy(d, q).wait_recv()
            total = total + ret2_in[d - 1, :, columns].astype(F32)
        out_ref[:, columns] = total.astype(BF16)

    for d in range(1, n_attn):
        ids_send(d, me).wait_send()
        gw_send(d, me).wait_send()
    for q in range(TOKEN_CUTS):
        near(0, q, me).wait_send()
        for d in range(1, lines):
            far(d, q, me).wait_send()
            near(d, q, sender(d)).wait_send()
    for q in range(RETURN_CUTS):
        ret1_copy(q).wait_send()
        for d in range(1, lines):
            ret2_copy(d, q).wait_send()

    for way in range(2):
        for j in range(local):
            @pl.when(steps_from(way) < last)
            def _():
                remote(part.at[j, way], part_in.at[j, way], part_s.at[way, j], part_r.at[way, 0],
                       "expert", lax.rem(mine + 1 - 2 * way + n_exp, n_exp)).wait_send()

            @pl.when(steps_from(way) > 0)
            def _():
                remote(hid.at[j, way], hid.at[j, way], hid_s.at[way, j], hid_r.at[way, 0],
                       "expert", lax.rem(mine - 1 + 2 * way + n_exp, n_exp)).wait_send()


def routed(tokens, expert_ids, gate_weight, w_gate, w_up, w_down, query, cache_k, cache_v, lengths, n_attn, n_exp):
    rows, feat = tokens.shape
    local, _, ffn = w_gate.shape
    feat_out = w_down.shape[2]
    topk = expert_ids.shape[1]
    experts = local * n_attn
    capacity = rows * topk // local
    half = capacity // 2
    lines = n_attn // 2
    chunks = local * (half // CHUNK_ROWS)
    seqs, heads, size = query.shape
    context, kv_count = cache_k.shape[1:3]
    flat = (seqs, context * kv_count, size)
    dma = pltpu.SemaphoreType.DMA
    vmem = pltpu.VMEM
    return pl.pallas_call(
        functools.partial(moe_kernel, n_attn, n_exp, experts, kv_count),
        out_shape=(
            jax.ShapeDtypeStruct((rows, feat_out), BF16),
            jax.ShapeDtypeStruct(query.shape, BF16),
        ),
        in_specs=[pl.BlockSpec(memory_space=pltpu.HBM)] * 10,
        out_specs=[pl.BlockSpec(memory_space=pltpu.VMEM)] * 2,
        scratch_shapes=[
            vmem(w_gate.shape, BF16),
            vmem(w_up.shape, BF16),
            vmem(w_down.shape, BF16),
            vmem(flat, BF16),
            vmem(flat, BF16),
            vmem(query.shape, BF16),
            pltpu.SMEM(lengths.shape, I32),
            vmem((n_attn, rows, feat), BF16),
            vmem((n_attn, topk, rows), I32),
            vmem((n_attn, topk, rows), BF16),
            vmem((experts, n_attn * rows), I32),
            vmem((experts, n_attn * rows), F32),
            vmem((local, 2, half, 2 * ffn), BF16),
            vmem((local, 2, half, 2 * ffn), BF16),
            vmem((local, 2, half, ffn), BF16),
            vmem((n_attn * rows, feat_out), F32),
            vmem((lines, rows, feat_out), BF16),
            vmem((lines, rows, feat_out), BF16),
            vmem((lines - 1, rows, feat_out), BF16),
            vmem((lines - 1, rows, feat_out), BF16),
            dma((3, local)),
            dma((7,)),
            dma((n_attn - 1,)),
            dma((n_attn - 1,)),
            dma((n_attn - 1,)),
            dma((n_attn - 1,)),
            dma((lines - 1, TOKEN_CUTS)),
            dma((lines - 1, TOKEN_CUTS)),
            dma((lines, TOKEN_CUTS)),
            dma((lines, TOKEN_CUTS)),
            dma((2, local)),
            dma((2, chunks)),
            dma((2, local)),
            dma((2, chunks)),
            dma((RETURN_CUTS,)),
            dma((RETURN_CUTS,)),
            dma((lines - 1, RETURN_CUTS)),
            dma((lines - 1, RETURN_CUTS)),
        ],
        compiler_params=pltpu.CompilerParams(
            collective_id=0, has_side_effects=True, vmem_limit_bytes=56 * 1024 * 1024
        ),
    )(
        tokens, expert_ids.T, gate_weight.T, w_gate, w_up, w_down, lengths, query,
        cache_k.reshape(flat), cache_v.reshape(flat),
    )


def body(tokens, expert_ids, gate_weight, w_gate, w_up, w_down, query, cache_k, cache_v, lengths):
    n_attn = lax.axis_size("attn")
    n_exp = lax.axis_size("expert")
    moe_out, attended = routed(
        tokens, expert_ids, gate_weight, w_gate, w_up, w_down,
        query, cache_k, cache_v, lengths, n_attn, n_exp,
    )
    attn_out = attended.reshape(query.shape[0], -1)
    return (moe_out, attn_out)


def solution(mesh):
    return jax.shard_map(
        body,
        mesh=mesh,
        in_specs=(
            P(("groups", "attn"), "expert"),
            P(("groups", "attn"), None),
            P(("groups", "attn"), None),
            P("attn", "expert", None),
            P("attn", "expert", None),
            P("attn", None, "expert"),
            P(("groups", "attn", "expert"), None, None),
            P(("groups", "attn", "expert"), None, None, None),
            P(("groups", "attn", "expert"), None, None, None),
            P(("groups", "attn", "expert")),
        ),
        out_specs=(P(("groups", "attn"), "expert"), P(("groups", "attn", "expert"), None)),
        check_vma=False,
    )
```

time: 114 us -> 255 us (2.24)
  Pallas kernels: 106 us -> 251 us
    pallas_call x1, Pallas kernels: 106 us -> 251 us  [routed(): pl.pallas_call(functools.partial(moe_kernel, n_attn, n_exp, experts, kv_c...]
where the time goes in v1:
time: 255 us; the launch traced here: 254 us
  Pallas kernels  251 us (98%)
  local copies, waits for them, and re-layouts  3.08 us (1%)
    pallas_call x1, Pallas kernels, routed(): pl.pallas_call(functools.partial(moe_kernel, n_attn, n_exp, experts, kv_c...  251 us

profile of v1, /device:TPU:1, one launch (start us, length us, event | category | flops | bytes accessed | tf_op | source)
XLA Modules:
  0.0 254.4 jit_solution(3886337369364997464)
XLA Ops:
  0.6 250.7 %shard_map.113 = (bf16[128,1024]{1,0:T(8,128)(2,1)}, bf16[2,64,128]{2,1,0:T(8,128)(2,1)}) custom-call(bf16[128,1024]{1,0:T(8,128)(2,1)} %tok_hbm.1, s32[8,128]{1,0:T(8,128)} %bitcast.12, bf16[8,128]{1,0:T(8,128)(2,1)} %bitcast.13, bf16[4,1024,768]{2,1,0:T(8,128)(2,1)} %wg_hbm.1, bf16[4,1024,768]{2,1,0:T(8,128)(2,1)} %wu_hbm.1, bf16[4,768,1024]{2,1,0:T(8,128)(2,1)} %wd_hbm.1, ...), custom_call_target="tpu_custom_call" | custom-call | tf_op jit(solution)/shard_map/pallas_call | solution.py:424
  251.3 1.4 copy.14
  252.7 1.7 copy.16

commit v2 on v1

--- a/solution.py
+++ b/solution.py
@@ -14,7 +14,11 @@
 TOKEN_CUTS = 4
 CHUNK_ROWS = 16
 LAG = 3
+HLAG = 8
+PACE = 2
+FIRST_STEPS = 1
 RETURN_CUTS = 4
+RETURN_DELAY = 2
 
 
 def remote(src, dst, send_sem, recv_sem, axis, peer):
@@ -61,6 +65,8 @@
     query_hbm,
     ck_hbm,
     cv_hbm,
+    out_hbm,
+    att_hbm,
     out_ref,
     att_ref,
     wg,
@@ -79,12 +85,16 @@
     part_in,
     hid,
     acc,
+    final,
+    early,
+    res,
     ret1,
     ret1_in,
     ret2,
     ret2_in,
     w_sem,
     c_sem,
+    out_sem,
     ids_s,
     ids_r,
     gw_s,
@@ -125,25 +135,15 @@
     def at_line(other):
         return lax.rem(other + 2 * lines, lines)
 
-    tok_copy = pltpu.make_async_copy(tok_hbm, tok_all.at[me], c_sem.at[0])
+    tok_copy = pltpu.make_async_copy(tok_hbm, tok_all.at[lines + line], c_sem.at[0])
     ids_copy = pltpu.make_async_copy(ids_hbm, ids_all.at[me], c_sem.at[1])
     gw_copy = pltpu.make_async_copy(gw_hbm, gw_all.at[me], c_sem.at[2])
     len_copy = pltpu.make_async_copy(length_hbm, length, c_sem.at[3])
     query_copy = pltpu.make_async_copy(query_hbm, query, c_sem.at[4])
     ck_copy = pltpu.make_async_copy(ck_hbm, ck, c_sem.at[5])
     cv_copy = pltpu.make_async_copy(cv_hbm, cv, c_sem.at[6])
-    for copy in (ids_copy, gw_copy, tok_copy, len_copy, query_copy, ck_copy, cv_copy):
+    for copy in (ids_copy, gw_copy, tok_copy):
         copy.start()
-
-    def weight_copy(i, j):
-        src, dst = ((wg_hbm, wg), (wu_hbm, wu), (wd_hbm, wd))[i]
-        return pltpu.make_async_copy(src.at[j], dst.at[j], w_sem.at[i, j])
-
-    for j in range(local):
-        weight_copy(0, j).start()
-        weight_copy(1, j).start()
-    for j in range(local):
-        weight_copy(2, j).start()
 
     barrier = pltpu.get_barrier_semaphore()
     for d in range(1, n_attn):
@@ -170,6 +170,19 @@
     ids_copy.wait()
     gw_copy.wait()
     tok_copy.wait()
+    for copy in (query_copy, len_copy, ck_copy, cv_copy):
+        copy.start()
+
+    def weight_copy(i, j):
+        src, dst = ((wg_hbm, wg), (wu_hbm, wu), (wd_hbm, wd))[i]
+        return pltpu.make_async_copy(src.at[j], dst.at[j], w_sem.at[i, j])
+
+    for j in range(local):
+        weight_copy(0, j).start()
+        weight_copy(1, j).start()
+    for j in range(local):
+        weight_copy(2, j).start()
+
     pl.semaphore_wait(barrier, n_attn - 1 + ends)
 
     def ids_send(d, slot):
@@ -181,25 +194,24 @@
                       "attn", lax.rem(me + d, n_attn))
 
     def far(d, q, block):
-        view = tok_all.at[block, :, pl.ds(q * cut, cut)]
+        view = tok_all.at[lines + block, :, pl.ds(q * cut, cut)]
         return remote(view, view, far_s.at[d - 1, q], far_r.at[d - 1, q],
                       "attn", at_line(line + d) * 2 + lane)
 
-    def near(d, q, block):
-        view = tok_all.at[block, :, pl.ds(q * cut, cut)]
-        return remote(view, view, near_s.at[d, q], near_r.at[d, q], "attn", partner)
-
-    def sender(d):
-        return at_line(line - d) * 2 + lane
+    def near(d, q):
+        block = at_line(line - d)
+        columns = pl.ds(q * cut, cut)
+        return remote(tok_all.at[lines + block, :, columns], tok_all.at[block, :, columns],
+                      near_s.at[d, q], near_r.at[d, q], "attn", partner)
 
     for d in range(1, n_attn):
         ids_send(d, me).start()
         gw_send(d, me).start()
     for q in range(TOKEN_CUTS):
         for d in range(1, lines):
-            far(d, q, me).start()
+            far(d, q, line).start()
     for q in range(TOKEN_CUTS):
-        near(0, q, me).start()
+        near(0, q).start()
 
     acc[...] = jnp.zeros_like(acc)
 
@@ -223,29 +235,59 @@
             factor = jnp.where(hit, wide[k:k + 1, :], factor)
         place = jnp.dot(member.astype(BF16), before, preferred_element_type=F32) + offset
         offset = offset + jnp.sum(member, axis=1, keepdims=True)
-        pos[:, b * rows:(b + 1) * rows] = jnp.where(member > 0.5, place, -1.0).astype(I32)
-        gate_of[:, b * rows:(b + 1) * rows] = factor
+        here = lax.rem(b + lane + 1, 2) * lines + b // 2
+        columns = pl.ds(pl.multiple_of(here * rows, rows), rows)
+        pos[:, columns] = jnp.where(member > 0.5, place, -1.0).astype(I32)
+        gate_of[:, columns] = factor
 
     len_copy.wait()
     query_copy.wait()
     ck_copy.wait()
     cv_copy.wait()
-    relay = [(d, q) for q in range(TOKEN_CUTS) for d in range(1, lines)]
+    def relay(q):
+        for d in range(1, lines):
+            far(d, q, at_line(line - d)).wait_recv()
+            near(d, q).start()
+
+    def chosen_of(j):
+        place = pos[pl.ds(me * local + j, 1), :]
+        slots = lax.broadcasted_iota(I32, (capacity, all_rows), 0)
+        return (slots == place).astype(F32).astype(BF16)
+
+    def start_first(q):
+        for d in range(lines):
+            near(d, q).wait_recv()
+        columns = slice(q * cut, (q + 1) * cut)
+        packed = jnp.dot(
+            final[...], tok_all[:, :, columns].reshape(all_rows, cut),
+            preferred_element_type=F32,
+        ).astype(BF16)
+        for w, to in ((wg, 0), (wu, ffn)):
+            term = jnp.dot(packed, w[0, columns, :], preferred_element_type=F32)
+            if q > 0:
+                term = term + early[:, to:to + ffn]
+            if q < TOKEN_CUTS - 1:
+                early[:, to:to + ffn] = term
+            else:
+                part[0, :, :, to:to + ffn] = term.astype(BF16).reshape(2, half, ffn)
+
+    final[...] = chosen_of(0)
     seqs = query.shape[0]
-    done = 0
-    for s in range(seqs):
-        attend(s, length[s], query, ck, cv, att_ref, kv_count)
-        until = len(relay) * (s + 1) // (seqs + 1)
-        for d, q in relay[done:until]:
-            far(d, q, sender(d)).wait_recv()
-            near(d, q, sender(d)).start()
-        done = until
-    for d, q in relay[done:]:
-        far(d, q, sender(d)).wait_recv()
-        near(d, q, sender(d)).start()
     for q in range(TOKEN_CUTS):
-        for d in range(lines):
-            near(d, q, at_line(line - d) * 2 + 1 - lane).wait_recv()
+        relay(q)
+        for s in range(seqs):
+            if s * (TOKEN_CUTS - 1) // seqs == q:
+                attend(s, length[s], query, ck, cv, att_ref, kv_count)
+        if q == TOKEN_CUTS - 2:
+            weight_copy(0, 0).wait()
+            weight_copy(1, 0).wait()
+            for r in range(q):
+                start_first(r)
+    for q in range(max(TOKEN_CUTS - 2, 0), TOKEN_CUTS):
+        start_first(q)
+
+    att_copy = pltpu.make_async_copy(att_ref, att_hbm, c_sem.at[7])
+    att_copy.start()
 
     def steps_from(way):
         return mine if way == 0 else last - mine
@@ -265,12 +307,16 @@
                       hid_s.at[way, k // per], hid_r.at[way, k],
                       "expert", lax.rem(mine - 1 + 2 * way + n_exp, n_exp))
 
+    def send_parts(j):
+        for way in range(2):
+            @pl.when(steps_from(way) == 0)
+            def _():
+                for r in range(per):
+                    part_copy(way, j * per + r).start()
+
     def first(j, carry):
-        place = pos[pl.ds(me * local + j, 1), :]
-        chosen = lax.broadcasted_iota(I32, (capacity, all_rows), 0) == place
         packed = jnp.dot(
-            chosen.astype(F32).astype(BF16),
-            tok_all[...].reshape(all_rows, feat),
+            chosen_of(j), tok_all[...].reshape(all_rows, feat),
             preferred_element_type=F32,
         ).astype(BF16)
         weight_copy(0, j).wait()
@@ -279,14 +325,11 @@
         part[j, :, :, :ffn] = gate.reshape(2, half, ffn)
         up = jnp.dot(packed, wu[j], preferred_element_type=F32).astype(BF16)
         part[j, :, :, ffn:] = up.reshape(2, half, ffn)
-        for way in range(2):
-            @pl.when(steps_from(way) == 0)
-            def _():
-                for r in range(per):
-                    part_copy(way, j * per + r).start()
+        send_parts(j)
         return carry
 
-    lax.fori_loop(0, local, first, 0)
+    send_parts(0)
+    lax.fori_loop(1, local - 1, first, 0)
 
     def reduce(way, k):
         part_copy(way, k).wait_recv()
@@ -314,42 +357,67 @@
                 reduce(way, k)
         return carry
 
-    lax.fori_loop(0, chunks + LAG * (last - 1), reduce_step, 0)
-
-    def pass_on(k, carry):
+    def pass_on(s, carry):
         for way in range(2):
-            @pl.when(steps_from(way) < last)
+            hops = last - steps_from(way)
+            k = s - HLAG * (hops - 1)
+            due = (hops > 0) & (k >= 0) & (k < chunks)
+
+            @pl.when(due)
             def _():
                 hid_copy(way, k).wait_recv()
 
-            @pl.when((steps_from(way) < last) & (steps_from(way) > 0))
+            @pl.when(due & (hops < last))
             def _():
                 hid_copy(way, k).start()
         return carry
 
+    ahead = HLAG * (last - 1)
+    over = LAG * (last - 1)
+
+    def both_steps(s, carry):
+        reduce_step(s, carry)
+        for i in range(PACE):
+            pass_on((s - chunks) * PACE + i, carry)
+        return carry
+
+    lax.fori_loop(0, FIRST_STEPS, reduce_step, 0)
+    first(local - 1, 0)
+    lax.fori_loop(FIRST_STEPS, chunks, reduce_step, 0)
+    lax.fori_loop(chunks, chunks + over, both_steps, 0)
+    lax.fori_loop(min(over * PACE, ahead), ahead, pass_on, 0)
+
+    def spread_of(j):
+        place = pos[pl.ds(me * local + j, 1), :]
+        factor = gate_of[pl.ds(me * local + j, 1), :]
+        slots = lax.broadcasted_iota(I32, (capacity, all_rows), 0)
+        return jnp.where(slots == place, factor, 0.0).astype(BF16)
+
+    def combine(spread, result):
+        return lax.dot_general(
+            spread, result, (((0,), (0,)), ((), ())), preferred_element_type=F32
+        )
+
     def second(j, carry):
-        lax.fori_loop(j * per, (j + 1) * per, pass_on, 0)
+        lax.fori_loop(jnp.maximum(ahead + j * per, over * PACE), ahead + (j + 1) * per, pass_on, 0)
         weight_copy(2, j).wait()
         result = jnp.dot(
             hid[j].reshape(capacity, ffn), wd[j], preferred_element_type=F32
         ).astype(BF16)
-        place = pos[pl.ds(me * local + j, 1), :]
-        factor = gate_of[pl.ds(me * local + j, 1), :]
-        slots = lax.broadcasted_iota(I32, (capacity, all_rows), 0)
-        spread = jnp.where(slots == place, factor, 0.0).astype(BF16)
-        acc[...] += lax.dot_general(
-            spread, result, (((0,), (0,)), ((), ())), preferred_element_type=F32
-        )
+        acc[...] += combine(spread_of(j), result)
         return carry
 
-    lax.fori_loop(0, local, second, 0)
-
-    def block(index, q):
-        return acc[pl.ds(pl.multiple_of(index * rows, rows), rows), q * out_cut:(q + 1) * out_cut]
+    lax.fori_loop(0, local - 1, second, 0)
+    j = local - 1
+    weight_copy(2, j).wait()
+    final[...] = spread_of(j)
+    lax.fori_loop(ahead + j * per, ahead + (j + 1) * per, pass_on, 0)
+
+    split = all_rows // 2
 
     def ret1_copy(q):
         columns = pl.ds(q * out_cut, out_cut)
-        return remote(ret1.at[:, :, columns], ret1_in.at[:, :, columns],
+        return remote(ret1.at[:, columns], ret1_in.at[:, columns],
                       ret1_s.at[q], ret1_r.at[q], "attn", partner)
 
     def ret2_copy(d, q):
@@ -358,40 +426,69 @@
                       ret2_s.at[d - 1, q], ret2_r.at[d - 1, q],
                       "attn", at_line(line + d) * 2 + lane)
 
-    for q in range(RETURN_CUTS):
-        columns = slice(q * out_cut, (q + 1) * out_cut)
-        for y in range(lines):
-            ret1[y, :, columns] = block(2 * y + 1 - lane, q).astype(BF16)
+    def columns_of(q):
+        return slice(q * out_cut, (q + 1) * out_cut)
+
+    def own(index, q):
+        return pl.ds(pl.multiple_of(split + index * rows, rows), rows), columns_of(q)
+
+    def got(index, q):
+        return pl.ds(pl.multiple_of(index * rows, rows), rows), columns_of(q)
+
+    def to_partner(q):
+        columns = columns_of(q)
+        result = jnp.dot(
+            hid[j].reshape(capacity, ffn), wd[j, :, columns], preferred_element_type=F32
+        ).astype(BF16)
+        res[:, columns] = result
+        ret1[:, columns] = (acc[:split, columns] + combine(final[:, :split], result)).astype(BF16)
         ret1_copy(q).start()
-    for q in range(RETURN_CUTS):
-        columns = slice(q * out_cut, (q + 1) * out_cut)
+
+    def to_lines(q):
+        columns = columns_of(q)
+        acc[split:, columns] += combine(final[:, split:], res[:, columns])
         ret1_copy(q).wait_recv()
         for d in range(1, lines):
             to = at_line(line + d)
             ret2[d - 1, :, columns] = (
-                block(2 * to + lane, q) + ret1_in[to, :, columns].astype(F32)
+                acc[own(to, q)] + ret1_in[got(to, q)].astype(F32)
             ).astype(BF16)
             ret2_copy(d, q).start()
+
     for q in range(RETURN_CUTS):
-        columns = slice(q * out_cut, (q + 1) * out_cut)
-        total = block(me, q) + ret1_in[line, :, columns].astype(F32)
+        to_partner(q)
+        if q >= RETURN_DELAY:
+            to_lines(q - RETURN_DELAY)
+    for q in range(max(RETURN_CUTS - RETURN_DELAY, 0), RETURN_CUTS):
+        to_lines(q)
+    def out_copy(q):
+        columns = pl.ds(q * out_cut, out_cut)
+        return pltpu.make_async_copy(out_ref.at[:, columns], out_hbm.at[:, columns], out_sem.at[q])
+
+    for q in range(RETURN_CUTS):
+        total = acc[own(line, q)] + ret1_in[got(line, q)].astype(F32)
         for d in range(1, lines):
             ret2_copy(d, q).wait_recv()
-            total = total + ret2_in[d - 1, :, columns].astype(F32)
-        out_ref[:, columns] = total.astype(BF16)
+            total = total + ret2_in[d - 1, :, columns_of(q)].astype(F32)
+        out_ref[:, columns_of(q)] = total.astype(BF16)
+        out_copy(q).start()
 
     for d in range(1, n_attn):
         ids_send(d, me).wait_send()
         gw_send(d, me).wait_send()
     for q in range(TOKEN_CUTS):
-        near(0, q, me).wait_send()
+        near(0, q).wait_send()
         for d in range(1, lines):
-            far(d, q, me).wait_send()
-            near(d, q, sender(d)).wait_send()
+            far(d, q, line).wait_send()
+            near(d, q).wait_send()
     for q in range(RETURN_CUTS):
         ret1_copy(q).wait_send()
         for d in range(1, lines):
             ret2_copy(d, q).wait_send()
+
+    att_copy.wait()
+    for q in range(RETURN_CUTS):
+        out_copy(q).wait()
 
     for way in range(2):
         for j in range(local):
@@ -428,8 +525,10 @@
             jax.ShapeDtypeStruct(query.shape, BF16),
         ),
         in_specs=[pl.BlockSpec(memory_space=pltpu.HBM)] * 10,
-        out_specs=[pl.BlockSpec(memory_space=pltpu.VMEM)] * 2,
+        out_specs=[pl.BlockSpec(memory_space=pltpu.HBM)] * 2,
         scratch_shapes=[
+            vmem((rows, feat_out), BF16),
+            vmem(query.shape, BF16),
             vmem(w_gate.shape, BF16),
             vmem(w_up.shape, BF16),
             vmem(w_down.shape, BF16),
@@ -446,12 +545,16 @@
             vmem((local, 2, half, 2 * ffn), BF16),
             vmem((local, 2, half, ffn), BF16),
             vmem((n_attn * rows, feat_out), F32),
-            vmem((lines, rows, feat_out), BF16),
-            vmem((lines, rows, feat_out), BF16),
+            vmem((capacity, n_attn * rows), BF16),
+            vmem((capacity, 2 * ffn), F32),
+            vmem((capacity, feat_out), BF16),
+            vmem((lines * rows, feat_out), BF16),
+            vmem((lines * rows, feat_out), BF16),
             vmem((lines - 1, rows, feat_out), BF16),
             vmem((lines - 1, rows, feat_out), BF16),
             dma((3, local)),
-            dma((7,)),
+            dma((8,)),
+            dma((RETURN_CUTS,)),
             dma((n_attn - 1,)),
             dma((n_attn - 1,)),
             dma((n_attn - 1,)),
@@ -478,6 +581,26 @@
     )
 
 
+def finish_kernel(moe_ref, att_ref, out_ref, attn_out_ref):
+    heads, size = att_ref.shape[1:]
+    out_ref[...] = moe_ref[...]
+    for h in range(heads):
+        attn_out_ref[:, h * size:(h + 1) * size] = att_ref[:, h, :]
+
+
+def finish(moe, att):
+    seqs, heads, size = att.shape
+    return pl.pallas_call(
+        finish_kernel,
+        out_shape=(
+            jax.ShapeDtypeStruct(moe.shape, moe.dtype),
+            jax.ShapeDtypeStruct((seqs, heads * size), att.dtype),
+        ),
+        in_specs=[pl.BlockSpec(memory_space=pltpu.VMEM)] * 2,
+        out_specs=[pl.BlockSpec(memory_space=pltpu.VMEM)] * 2,
+    )(moe, att)
+
+
 def body(tokens, expert_ids, gate_weight, w_gate, w_up, w_down, query, cache_k, cache_v, lengths):
     n_attn = lax.axis_size("attn")
     n_exp = lax.axis_size("expert")
@@ -485,8 +608,7 @@
         tokens, expert_ids, gate_weight, w_gate, w_up, w_down,
         query, cache_k, cache_v, lengths, n_attn, n_exp,
     )
-    attn_out = attended.reshape(query.shape[0], -1)
-    return (moe_out, attn_out)
+    return finish(moe_out, attended)
 
 
 def solution(mesh):

time: 255 us -> 89.9 us (0.35)
  Pallas kernels: 251 us -> 88.1 us
  local copies, waits for them, and re-layouts: 3.08 us -> 0 us
    pallas_call x1, Pallas kernels: 251 us -> 86.4 us  [routed(): pl.pallas_call(functools.partial(moe_kernel, n_attn, n_exp, experts, kv_c...]
    unnamed x2 -> x0, local copies, waits for them, and re-layouts: 3.08 us -> none
where the time goes in v2:
time: 89.9 us; the launch traced here: 88.7 us
  Pallas kernels  88.1 us (98%)
    pallas_call x1, Pallas kernels, routed(): pl.pallas_call(functools.partial(moe_kernel, n_attn, n_exp, experts, kv_c...  86.4 us

profile of v2, /device:TPU:1, one launch (start us, length us, event | category | flops | bytes accessed | tf_op | source)
XLA Modules:
  0.0 88.7 jit_solution(6924480768491414427)
XLA Ops:
  0.6 86.4 %shard_map.113 = (bf16[128,1024]{1,0:T(8,128)(2,1)}, bf16[2,64,128]{2,1,0:T(8,128)(2,1)}) custom-call(bf16[128,1024]{1,0:T(8,128)(2,1)} %tok_hbm.1, s32[8,128]{1,0:T(8,128)} %bitcast.6, bf16[8,128]{1,0:T(8,128)(2,1)} %bitcast.7, bf16[4,1024,768]{2,1,0:T(8,128)(2,1)} %wg_hbm.1, bf16[4,1024,768]{2,1,0:T(8,128)(2,1)} %wu_hbm.1, bf16[4,768,1024]{2,1,0:T(8,128)(2,1)} %wd_hbm.1, ...), custom_call_target="tpu_custom_call" | custom-call | tf_op jit(solution)/shard_map/pallas_call | solution.py:521
  87.1 1.7 %shard_map.114 = (bf16[128,1024]{1,0:T(8,128)(2,1)}, bf16[2,8192]{1,0:T(2,128)(2,1)}) custom-call(bf16[128,1024]{1,0:T(8,128)(2,1)} %get-tuple-element.4.moe_ref, bf16[2,64,128]{2,1,0:T(8,128)(2,1)} %get-tuple-element.5.att_ref), custom_call_target="tpu_custom_call" | custom-call | tf_op jit(solution)/shard_map/pallas_call | solution.py:593

commit v3 on v2

--- a/solution.py
+++ b/solution.py
@@ -16,7 +16,6 @@
 LAG = 3
 HLAG = 8
 PACE = 2
-FIRST_STEPS = 1
 RETURN_CUTS = 4
 RETURN_DELAY = 2
 
@@ -85,6 +84,7 @@
     part_in,
     hid,
     acc,
+    chosen,
     final,
     early,
     res,
@@ -106,7 +106,6 @@
     part_s,
     part_r,
     hid_s,
-    hid_r,
     ret1_s,
     ret1_r,
     ret2_s,
@@ -240,10 +239,12 @@
         pos[:, columns] = jnp.where(member > 0.5, place, -1.0).astype(I32)
         gate_of[:, columns] = factor
 
-    len_copy.wait()
-    query_copy.wait()
-    ck_copy.wait()
-    cv_copy.wait()
+    def spread_of(j):
+        place = pos[pl.ds(me * local + j, 1), :]
+        factor = gate_of[pl.ds(me * local + j, 1), :]
+        slots = lax.broadcasted_iota(I32, (capacity, all_rows), 0)
+        return jnp.where(slots == place, factor, 0.0)
+
     def relay(q):
         for d in range(1, lines):
             far(d, q, at_line(line - d)).wait_recv()
@@ -259,7 +260,7 @@
             near(d, q).wait_recv()
         columns = slice(q * cut, (q + 1) * cut)
         packed = jnp.dot(
-            final[...], tok_all[:, :, columns].reshape(all_rows, cut),
+            chosen[...], tok_all[:, :, columns].reshape(all_rows, cut),
             preferred_element_type=F32,
         ).astype(BF16)
         for w, to in ((wg, 0), (wu, ffn)):
@@ -271,26 +272,20 @@
             else:
                 part[0, :, :, to:to + ffn] = term.astype(BF16).reshape(2, half, ffn)
 
-    final[...] = chosen_of(0)
-    seqs = query.shape[0]
-    for q in range(TOKEN_CUTS):
+    chosen[...] = chosen_of(0)
+    final[...] = spread_of(local - 1).T.astype(BF16)
+    relay(0)
+    weight_copy(0, 0).wait()
+    weight_copy(1, 0).wait()
+    for q in range(1, TOKEN_CUTS):
         relay(q)
-        for s in range(seqs):
-            if s * (TOKEN_CUTS - 1) // seqs == q:
-                attend(s, length[s], query, ck, cv, att_ref, kv_count)
-        if q == TOKEN_CUTS - 2:
-            weight_copy(0, 0).wait()
-            weight_copy(1, 0).wait()
-            for r in range(q):
-                start_first(r)
-    for q in range(max(TOKEN_CUTS - 2, 0), TOKEN_CUTS):
-        start_first(q)
-
-    att_copy = pltpu.make_async_copy(att_ref, att_hbm, c_sem.at[7])
-    att_copy.start()
+        start_first(q - 1)
+    start_first(TOKEN_CUTS - 1)
 
     def steps_from(way):
-        return mine if way == 0 else last - mine
+        return mine + way * (last - 2 * mine)
+
+    near_way = 2 * mine // n_exp
 
     def piece(ref, way, k):
         j = k // per
@@ -304,7 +299,7 @@
 
     def hid_copy(way, k):
         return remote(piece(hid, way, k), piece(hid, way, k),
-                      hid_s.at[way, k // per], hid_r.at[way, k],
+                      hid_s.at[way, k // per], part_r.at[way, k],
                       "expert", lax.rem(mine - 1 + 2 * way + n_exp, n_exp))
 
     def send_parts(j):
@@ -329,7 +324,7 @@
         return carry
 
     send_parts(0)
-    lax.fori_loop(1, local - 1, first, 0)
+    lax.fori_loop(1, local, first, 0)
 
     def reduce(way, k):
         part_copy(way, k).wait_recv()
@@ -349,7 +344,7 @@
             hid_copy(way, k).start()
 
     def reduce_step(s, carry):
-        for way in range(2):
+        for way in (near_way, 1 - near_way):
             k = s - LAG * (steps_from(way) - 1)
 
             @pl.when((steps_from(way) > 0) & (k >= 0) & (k < chunks))
@@ -358,7 +353,7 @@
         return carry
 
     def pass_on(s, carry):
-        for way in range(2):
+        for way in (1 - near_way, near_way):
             hops = last - steps_from(way)
             k = s - HLAG * (hops - 1)
             due = (hops > 0) & (k >= 0) & (k < chunks)
@@ -381,17 +376,9 @@
             pass_on((s - chunks) * PACE + i, carry)
         return carry
 
-    lax.fori_loop(0, FIRST_STEPS, reduce_step, 0)
-    first(local - 1, 0)
-    lax.fori_loop(FIRST_STEPS, chunks, reduce_step, 0)
+    lax.fori_loop(0, chunks, reduce_step, 0)
     lax.fori_loop(chunks, chunks + over, both_steps, 0)
     lax.fori_loop(min(over * PACE, ahead), ahead, pass_on, 0)
-
-    def spread_of(j):
-        place = pos[pl.ds(me * local + j, 1), :]
-        factor = gate_of[pl.ds(me * local + j, 1), :]
-        slots = lax.broadcasted_iota(I32, (capacity, all_rows), 0)
-        return jnp.where(slots == place, factor, 0.0).astype(BF16)
 
     def combine(spread, result):
         return lax.dot_general(
@@ -404,13 +391,12 @@
         result = jnp.dot(
             hid[j].reshape(capacity, ffn), wd[j], preferred_element_type=F32
         ).astype(BF16)
-        acc[...] += combine(spread_of(j), result)
+        acc[...] += combine(spread_of(j).astype(BF16), result)
         return carry
 
     lax.fori_loop(0, local - 1, second, 0)
     j = local - 1
     weight_copy(2, j).wait()
-    final[...] = spread_of(j)
     lax.fori_loop(ahead + j * per, ahead + (j + 1) * per, pass_on, 0)
 
     split = all_rows // 2
@@ -441,12 +427,14 @@
             hid[j].reshape(capacity, ffn), wd[j, :, columns], preferred_element_type=F32
         ).astype(BF16)
         res[:, columns] = result
-        ret1[:, columns] = (acc[:split, columns] + combine(final[:, :split], result)).astype(BF16)
+        ret1[:, columns] = (acc[:split, columns] + jnp.dot(final[:split], result, preferred_element_type=F32)).astype(BF16)
         ret1_copy(q).start()
 
     def to_lines(q):
         columns = columns_of(q)
-        acc[split:, columns] += combine(final[:, split:], res[:, columns])
+        acc[split:, columns] += jnp.dot(
+            final[split:], res[:, columns], preferred_element_type=F32
+        )
         ret1_copy(q).wait_recv()
         for d in range(1, lines):
             to = at_line(line + d)
@@ -461,6 +449,13 @@
             to_lines(q - RETURN_DELAY)
     for q in range(max(RETURN_CUTS - RETURN_DELAY, 0), RETURN_CUTS):
         to_lines(q)
+    att_copy = pltpu.make_async_copy(att_ref, att_hbm, c_sem.at[7])
+    for copy in (len_copy, query_copy, ck_copy, cv_copy):
+        copy.wait()
+    for s in range(query.shape[0]):
+        attend(s, length[s], query, ck, cv, att_ref, kv_count)
+    att_copy.start()
+
     def out_copy(q):
         columns = pl.ds(q * out_cut, out_cut)
         return pltpu.make_async_copy(out_ref.at[:, columns], out_hbm.at[:, columns], out_sem.at[q])
@@ -499,7 +494,7 @@
 
             @pl.when(steps_from(way) > 0)
             def _():
-                remote(hid.at[j, way], hid.at[j, way], hid_s.at[way, j], hid_r.at[way, 0],
+                remote(hid.at[j, way], hid.at[j, way], hid_s.at[way, j], part_r.at[way, 0],
                        "expert", lax.rem(mine - 1 + 2 * way + n_exp, n_exp)).wait_send()
 
 
@@ -546,6 +541,7 @@
             vmem((local, 2, half, ffn), BF16),
             vmem((n_attn * rows, feat_out), F32),
             vmem((capacity, n_attn * rows), BF16),
+            vmem((n_attn * rows, capacity), BF16),
             vmem((capacity, 2 * ffn), F32),
             vmem((capacity, feat_out), BF16),
             vmem((lines * rows, feat_out), BF16),
@@ -566,7 +562,6 @@
             dma((2, local)),
             dma((2, chunks)),
             dma((2, local)),
-            dma((2, chunks)),
             dma((RETURN_CUTS,)),
             dma((RETURN_CUTS,)),
             dma((lines - 1, RETURN_CUTS)),

time: 89.9 us -> 87.7 us (0.976)
  Pallas kernels: 88.1 us -> 85.8 us
    pallas_call x1, Pallas kernels: 86.4 us -> 84.2 us  [routed(): pl.pallas_call(functools.partial(moe_kernel, n_attn, n_exp, experts, kv_c...]
where the time goes in v3:
time: 87.7 us; the launch traced here: 86.5 us
  Pallas kernels  85.8 us (98%)
    pallas_call x1, Pallas kernels, routed(): pl.pallas_call(functools.partial(moe_kernel, n_attn, n_exp, experts, kv_c...  84.2 us

profile of v3, /device:TPU:1, one launch (start us, length us, event | category | flops | bytes accessed | tf_op | source)
XLA Modules:
  0.0 86.5 jit_solution(2050061559584337881)
XLA Ops:
  0.6 84.2 %shard_map.113 = (bf16[128,1024]{1,0:T(8,128)(2,1)}, bf16[2,64,128]{2,1,0:T(8,128)(2,1)}) custom-call(bf16[128,1024]{1,0:T(8,128)(2,1)} %tok_hbm.1, s32[8,128]{1,0:T(8,128)} %bitcast.6, bf16[8,128]{1,0:T(8,128)(2,1)} %bitcast.7, bf16[4,1024,768]{2,1,0:T(8,128)(2,1)} %wg_hbm.1, bf16[4,1024,768]{2,1,0:T(8,128)(2,1)} %wu_hbm.1, bf16[4,768,1024]{2,1,0:T(8,128)(2,1)} %wd_hbm.1, ...), custom_call_target="tpu_custom_call" | custom-call | tf_op jit(solution)/shard_map/pallas_call | solution.py:516
  84.8 1.7 %shard_map.114 = (bf16[128,1024]{1,0:T(8,128)(2,1)}, bf16[2,8192]{1,0:T(2,128)(2,1)}) custom-call(bf16[128,1024]{1,0:T(8,128)(2,1)} %get-tuple-element.4.moe_ref, bf16[2,64,128]{2,1,0:T(8,128)(2,1)} %get-tuple-element.5.att_ref), custom_call_target="tpu_custom_call" | custom-call | tf_op jit(solution)/shard_map/pallas_call | solution.py:588

commit v4 on v3

--- a/solution.py
+++ b/solution.py
@@ -17,7 +17,7 @@
 HLAG = 8
 PACE = 2
 RETURN_CUTS = 4
-RETURN_DELAY = 2
+RETURN_DELAY = 1
 
 
 def remote(src, dst, send_sem, recv_sem, axis, peer):
@@ -84,6 +84,7 @@
     part_in,
     hid,
     acc,
+    packed,
     chosen,
     final,
     early,
@@ -259,12 +260,12 @@
         for d in range(lines):
             near(d, q).wait_recv()
         columns = slice(q * cut, (q + 1) * cut)
-        packed = jnp.dot(
+        narrow = jnp.dot(
             chosen[...], tok_all[:, :, columns].reshape(all_rows, cut),
             preferred_element_type=F32,
         ).astype(BF16)
         for w, to in ((wg, 0), (wu, ffn)):
-            term = jnp.dot(packed, w[0, columns, :], preferred_element_type=F32)
+            term = jnp.dot(narrow, w[0, columns, :], preferred_element_type=F32)
             if q > 0:
                 term = term + early[:, to:to + ffn]
             if q < TOKEN_CUTS - 1:
@@ -309,22 +310,27 @@
                 for r in range(per):
                     part_copy(way, j * per + r).start()
 
-    def first(j, carry):
-        packed = jnp.dot(
+    def pack(j):
+        packed[...] = jnp.dot(
             chosen_of(j), tok_all[...].reshape(all_rows, feat),
             preferred_element_type=F32,
         ).astype(BF16)
-        weight_copy(0, j).wait()
-        weight_copy(1, j).wait()
-        gate = jnp.dot(packed, wg[j], preferred_element_type=F32).astype(BF16)
-        part[j, :, :, :ffn] = gate.reshape(2, half, ffn)
-        up = jnp.dot(packed, wu[j], preferred_element_type=F32).astype(BF16)
-        part[j, :, :, ffn:] = up.reshape(2, half, ffn)
+
+    def project(j, i):
+        weight_copy(i, j).wait()
+        w = (wg, wu)[i]
+        some = jnp.dot(packed[...], w[j], preferred_element_type=F32).astype(BF16)
+        part[j, :, :, i * ffn:(i + 1) * ffn] = some.reshape(2, half, ffn)
+
+    def first(j, carry):
+        pack(j)
+        project(j, 0)
+        project(j, 1)
         send_parts(j)
         return carry
 
     send_parts(0)
-    lax.fori_loop(1, local, first, 0)
+    lax.fori_loop(1, local - 1, first, 0)
 
     def reduce(way, k):
         part_copy(way, k).wait_recv()
@@ -376,7 +382,14 @@
             pass_on((s - chunks) * PACE + i, carry)
         return carry
 
-    lax.fori_loop(0, chunks, reduce_step, 0)
+    reduce_step(0, 0)
+    pack(local - 1)
+    reduce_step(1, 0)
+    project(local - 1, 0)
+    reduce_step(2, 0)
+    project(local - 1, 1)
+    send_parts(local - 1)
+    lax.fori_loop(3, chunks, reduce_step, 0)
     lax.fori_loop(chunks, chunks + over, both_steps, 0)
     lax.fori_loop(min(over * PACE, ahead), ahead, pass_on, 0)
 
@@ -540,6 +553,7 @@
             vmem((local, 2, half, 2 * ffn), BF16),
             vmem((local, 2, half, ffn), BF16),
             vmem((n_attn * rows, feat_out), F32),
+            vmem((capacity, feat), BF16),
             vmem((capacity, n_attn * rows), BF16),
             vmem((n_attn * rows, capacity), BF16),
             vmem((capacity, 2 * ffn), F32),

time: 87.7 us -> 87.3 us (level)
  no operation moved by 1% of the time
where the time goes in v4:
time: 87.3 us; the launch traced here: 86.6 us
  Pallas kernels  86 us (99%)
    pallas_call x1, Pallas kernels, routed(): pl.pallas_call(functools.partial(moe_kernel, n_attn, n_exp, experts, kv_c...  84.3 us

profile of v4, /device:TPU:1, one launch (start us, length us, event | category | flops | bytes accessed | tf_op | source)
XLA Modules:
  0.0 86.6 jit_solution(16086860849598031099)
XLA Ops:
  0.6 84.3 %shard_map.113 = (bf16[128,1024]{1,0:T(8,128)(2,1)}, bf16[2,64,128]{2,1,0:T(8,128)(2,1)}) custom-call(bf16[128,1024]{1,0:T(8,128)(2,1)} %tok_hbm.1, s32[8,128]{1,0:T(8,128)} %bitcast.6, bf16[8,128]{1,0:T(8,128)(2,1)} %bitcast.7, bf16[4,1024,768]{2,1,0:T(8,128)(2,1)} %wg_hbm.1, bf16[4,1024,768]{2,1,0:T(8,128)(2,1)} %wu_hbm.1, bf16[4,768,1024]{2,1,0:T(8,128)(2,1)} %wd_hbm.1, ...), custom_call_target="tpu_custom_call" | custom-call | tf_op jit(solution)/shard_map/pallas_call | solution.py:529
  85.0 1.7 %shard_map.114 = (bf16[128,1024]{1,0:T(8,128)(2,1)}, bf16[2,8192]{1,0:T(2,128)(2,1)}) custom-call(bf16[128,1024]{1,0:T(8,128)(2,1)} %get-tuple-element.4.moe_ref, bf16[2,64,128]{2,1,0:T(8,128)(2,1)} %get-tuple-element.5.att_ref), custom_call_target="tpu_custom_call" | custom-call | tf_op jit(solution)/shard_map/pallas_call | solution.py:602
